TPU v7x, 32 devices: a whole 2x2x4 slice. The times are simulated.
32 devices in a mesh: gx: 4 (over y, x), gy: 4 (over z), gz: 2 (over core).
Axes of the slice: x: 2, y: 2, z: 4, core: 2. Of those that a mesh axis runs over, the one named last changes fastest.
Arguments:
- blocks: int32 [32768, 4], P(('gx', 'gy', 'gz')), may hold values from 0 to 15, as said below
- coefficients: bfloat16 [32768, 4, 128], P(('gx', 'gy', 'gz')), may hold values from -80 to 80
- residuals: float32 [32768], P(('gx', 'gy', 'gz')), may hold values from -3000 to 3000
Outputs:
- factor: float32 [4, 4, 128, 4, 4, 128], P('gx', None, None, 'gy')
- solution: float32 [16, 128], replicated
Inputs may be any that keep to these rules, and one draw needn't show every extreme that they name: Each row names 4 different blocks.
All inputs are finite; a program needn't handle non-finite values.
Results may differ from a plain program's by a relative error of at most 0.0003.
Values sent between devices are 32-bit elements; how exact they have to be, the bound alone decides.
A program may use at most 128 MiB of HBM per device.

v0:
```python
import jax
import jax.numpy as jnp
from jax import lax
from jax.sharding import PartitionSpec as P

G = 2048
BS = 128


def from_root(block, axis, source):
    block = jnp.where(lax.axis_index(axis) == source, block, jnp.zeros_like(block))
    return lax.psum(block, axis)


def on_device(blocks, coefficients, residuals):
    row_count = lax.axis_size("gx")
    col_count = lax.axis_size("gy")
    row_index = lax.axis_index("gx")
    col_index = lax.axis_index("gy")
    scale = 1.0 / (coefficients.shape[0] * row_count * col_count * lax.axis_size("gz"))
    width = coefficients.shape[2]
    nblock = G // BS
    per_dev = nblock // row_count
    target = (
        jnp.arange(per_dev, dtype=jnp.int32)[None, :] * row_count
        + jnp.arange(row_count, dtype=jnp.int32)[:, None]
    ).reshape(-1)
    placed = (blocks[:, :, None] == target[None, None, :]).astype(jnp.bfloat16)
    design = jnp.einsum("osz,osx->ozx", placed, coefficients, preferred_element_type=jnp.float32)
    design = design.astype(jnp.bfloat16).reshape(-1, row_count, per_dev, width)
    natural = (blocks[:, :, None] == jnp.arange(nblock, dtype=jnp.int32)[None, None, :]).astype(
        jnp.float32
    )
    weighted = coefficients.astype(jnp.float32) * residuals[:, None, None]
    rhs_local = (
        jnp.einsum("osb,osx->bx", natural, weighted, precision=lax.Precision.HIGHEST) * scale
    )
    rhs = lax.psum(rhs_local, ("gx", "gy", "gz"))
    term = (
        jnp.einsum("opix,oqjy->pqixjy", design, design, preferred_element_type=jnp.float32) * scale
    )
    term = term.reshape(row_count * col_count, per_dev, width, per_dev, width)
    halves = lax.psum_scatter(term, "gz", scatter_dimension=2, tiled=True)
    halves = lax.psum_scatter(halves, ("gx", "gy"), scatter_dimension=0, tiled=True)
    summed = lax.all_gather(halves, "gz", axis=2, tiled=True)
    matrix = summed.reshape(per_dev, width, per_dev, width)
    zero = jnp.zeros((), jnp.int32)
    block_ids = (
        jnp.arange(per_dev, dtype=jnp.int32)[None, :] * row_count
        + jnp.arange(row_count, dtype=jnp.int32)[:, None]
    )

    def factor_step(step, state):
        working, factor, pivots = state
        step_row = step % row_count
        step_local_row = step // row_count
        step_col = step % col_count
        step_local_col = step // col_count
        column = lax.dynamic_slice(
            working, (zero, zero, step_local_col, zero), (per_dev, width, 1, width)
        ).reshape(per_dev, width, width)
        row_raw = from_root(column, "gy", step_col)
        whole = lax.all_gather(row_raw, "gx", axis=0, tiled=True).reshape(
            row_count, per_dev, width, width
        )
        own_diag = lax.dynamic_slice(
            whole, (step_row, step_local_row, zero, zero), (1, 1, width, width)
        ).reshape(width, width)
        chol = jnp.linalg.cholesky(own_diag)
        stacked = whole.transpose(3, 0, 1, 2).reshape(width, row_count * per_dev * width)
        solved = jax.scipy.linalg.solve_triangular(chol, stacked, lower=True)
        panel_all = solved.reshape(width, row_count, per_dev, width).transpose(1, 2, 3, 0)
        panel_all = jnp.where((block_ids > step)[:, :, None, None], panel_all, 0.0)
        row_panel = lax.dynamic_index_in_dim(panel_all, row_index, 0, keepdims=False)
        col_panel = lax.dynamic_index_in_dim(panel_all, col_index, 0, keepdims=False)
        working = working - jnp.einsum(
            "rxk,cyk->rxcy", row_panel, col_panel, precision=lax.Precision.HIGHEST
        )
        on_diag = (jnp.arange(per_dev, dtype=jnp.int32) == step_local_row) & (row_index == step_row)
        new_column = row_panel + jnp.where(on_diag[:, None, None], chol[None], 0.0)
        old_column = lax.dynamic_slice(
            factor, (zero, zero, step_local_col, zero), (per_dev, width, 1, width)
        ).reshape(per_dev, width, width)
        kept = jnp.where(col_index == step_col, new_column, old_column)
        factor = lax.dynamic_update_slice(
            factor, kept.reshape(per_dev, width, 1, width), (zero, zero, step_local_col, zero)
        )
        pivots = lax.dynamic_update_slice(pivots, chol[None], (step, zero, zero))
        return (working, factor, pivots)

    start_state = (matrix, jnp.zeros_like(matrix), jnp.zeros((nblock, width, width), jnp.float32))
    _, factor, pivots = lax.fori_loop(0, nblock, factor_step, start_state)
    shaped = factor.reshape(1, per_dev, width, 1, per_dev, width)
    across = lax.all_gather(shaped, "gy", axis=3, tiled=True)
    whole = lax.all_gather(across, "gx", axis=0, tiled=True)
    lower = whole.transpose(1, 0, 2, 4, 3, 5).reshape(nblock * width, nblock * width)
    middle = jax.scipy.linalg.solve_triangular(lower, rhs.reshape(-1), lower=True)
    answer = jax.scipy.linalg.solve_triangular(lower, middle, lower=True, trans=1)
    solution = answer.reshape(nblock, width)
    return (factor.reshape(1, per_dev, width, 1, per_dev, width), solution)


def solution(mesh):
    in_specs = (
        P(("gx", "gy", "gz"), None),
        P(("gx", "gy", "gz"), None, None),
        P(("gx", "gy", "gz")),
    )
    out_specs = (P("gx", None, None, "gy", None, None), P())
    return jax.shard_map(
        on_device, mesh=mesh, in_specs=in_specs, out_specs=out_specs, check_vma=False
    )
```

profile of v0, /device:TPU:0, one launch (start us, length us, event | category | flops | bytes accessed | tf_op | source)
XLA Modules:
  0.0 2390.0 jit_solution(993266467958038092)
XLA Ops:
  72.9 183.3 %reduce-scatter.5.cloned.1.call-done = f32[1,4,64,4,128]{4,2,3,1,0:T(8,128)} async-done(((f32[16,4,64,4,128]{4,2,3,1,0:T(8,128)}), f32[1,4,64,4,128]{4,2,3,1,0:T(8,128)}) %reduce-scatter.5.cloned.1.call-update) | async-done | bytes 524304 | tf_op jit(solution)/shard_map/reduce_scatter | solution.py:44
  266.6 1563.2 %while.20 = (s32[]{:T(128)}, f32[4,128,4,128]{3,1,2,0:T(8,128)}, f32[4,128,4,128]{3,1,2,0:T(8,128)S(1)}, s32[]{:T(128)}, s32[]{:T(128)}, /*index=5*/s32[]{:T(128...) while((s32[]{:T(128)}, f32[4,128,4,128]{3,1,2,0:T(8,128)}, ...), condition=%wide.region_6.7_spmd.clone, body=%wide.region_2.6_spmd.clone.sunk | while | flops 806305984 | bytes 14485572 | solution.py:92
  268.5 38.3 %all-reduce.2.cloned.1.call-done = f32[4,128,128]{2,1,0:T(8,128)} async-done(((f32[4,128,128]{2,1,0:T(8,128)}), f32[4,128,128]{2,1,0:T(8,128)}) %all-reduce.2.cloned.1.call-update) | async-done | bytes 262160 | tf_op jit(solution)/shard_map/while/body/eval_jaxpr/psum | solution.py:12
  367.0 37.2 %all-reduce.2.cloned.1.call-done = f32[4,128,128]{2,1,0:T(8,128)} async-done(((f32[4,128,128]{2,1,0:T(8,128)}), f32[4,128,128]{2,1,0:T(8,128)}) %all-reduce.2.cloned.1.call-update) | async-done | bytes 262160 | tf_op jit(solution)/shard_map/while/body/eval_jaxpr/psum | solution.py:12
  464.6 37.5 %all-reduce.2.cloned.1.call-done = f32[4,128,128]{2,1,0:T(8,128)} async-done(((f32[4,128,128]{2,1,0:T(8,128)}), f32[4,128,128]{2,1,0:T(8,128)}) %all-reduce.2.cloned.1.call-update) | async-done | bytes 262160 | tf_op jit(solution)/shard_map/while/body/eval_jaxpr/psum | solution.py:12
  562.5 37.2 %all-reduce.2.cloned.1.call-done = f32[4,128,128]{2,1,0:T(8,128)} async-done(((f32[4,128,128]{2,1,0:T(8,128)}), f32[4,128,128]{2,1,0:T(8,128)}) %all-reduce.2.cloned.1.call-update) | async-done | bytes 262160 | tf_op jit(solution)/shard_map/while/body/eval_jaxpr/psum | solution.py:12
  599.8 28.1 %all-gather.12.cloned.1.call-done = f32[16,128,128]{2,1,0:T(8,128)} async-done(((f32[4,128,128]{2,1,0:T(8,128)}), f32[16,128,128]{2,1,0:T(8,128)}) %all-gather.12.cloned.1.call-update) | async-done | bytes 1048592 | tf_op jit(solution)/shard_map/while/body/eval_jaxpr/all_gather | solution.py:63
  660.0 37.2 %all-reduce.2.cloned.1.call-done = f32[4,128,128]{2,1,0:T(8,128)} async-done(((f32[4,128,128]{2,1,0:T(8,128)}), f32[4,128,128]{2,1,0:T(8,128)}) %all-reduce.2.cloned.1.call-update) | async-done | bytes 262160 | tf_op jit(solution)/shard_map/while/body/eval_jaxpr/psum | solution.py:12
  757.6 37.2 %all-reduce.2.cloned.1.call-done = f32[4,128,128]{2,1,0:T(8,128)} async-done(((f32[4,128,128]{2,1,0:T(8,128)}), f32[4,128,128]{2,1,0:T(8,128)}) %all-reduce.2.cloned.1.call-update) | async-done | bytes 262160 | tf_op jit(solution)/shard_map/while/body/eval_jaxpr/psum | solution.py:12
  855.0 37.2 %all-reduce.2.cloned.1.call-done = f32[4,128,128]{2,1,0:T(8,128)} async-done(((f32[4,128,128]{2,1,0:T(8,128)}), f32[4,128,128]{2,1,0:T(8,128)}) %all-reduce.2.cloned.1.call-update) | async-done | bytes 262160 | tf_op jit(solution)/shard_map/while/body/eval_jaxpr/psum | solution.py:12
  952.5 37.2 %all-reduce.2.cloned.1.call-done = f32[4,128,128]{2,1,0:T(8,128)} async-done(((f32[4,128,128]{2,1,0:T(8,128)}), f32[4,128,128]{2,1,0:T(8,128)}) %all-reduce.2.cloned.1.call-update) | async-done | bytes 262160 | tf_op jit(solution)/shard_map/while/body/eval_jaxpr/psum | solution.py:12
  1050.0 37.2 %all-reduce.2.cloned.1.call-done = f32[4,128,128]{2,1,0:T(8,128)} async-done(((f32[4,128,128]{2,1,0:T(8,128)}), f32[4,128,128]{2,1,0:T(8,128)}) %all-reduce.2.cloned.1.call-update) | async-done | bytes 262160 | tf_op jit(solution)/shard_map/while/body/eval_jaxpr/psum | solution.py:12
  1147.6 37.5 %all-reduce.2.cloned.1.call-done = f32[4,128,128]{2,1,0:T(8,128)} async-done(((f32[4,128,128]{2,1,0:T(8,128)}), f32[4,128,128]{2,1,0:T(8,128)}) %all-reduce.2.cloned.1.call-update) | async-done | bytes 262160 | tf_op jit(solution)/shard_map/while/body/eval_jaxpr/psum | solution.py:12
  1245.5 37.2 %all-reduce.2.cloned.1.call-done = f32[4,128,128]{2,1,0:T(8,128)} async-done(((f32[4,128,128]{2,1,0:T(8,128)}), f32[4,128,128]{2,1,0:T(8,128)}) %all-reduce.2.cloned.1.call-update) | async-done | bytes 262160 | tf_op jit(solution)/shard_map/while/body/eval_jaxpr/psum | solution.py:12
  1343.1 37.2 %all-reduce.2.cloned.1.call-done = f32[4,128,128]{2,1,0:T(8,128)} async-done(((f32[4,128,128]{2,1,0:T(8,128)}), f32[4,128,128]{2,1,0:T(8,128)}) %all-reduce.2.cloned.1.call-update) | async-done | bytes 262160 | tf_op jit(solution)/shard_map/while/body/eval_jaxpr/psum | solution.py:12
  1440.5 37.5 %all-reduce.2.cloned.1.call-done = f32[4,128,128]{2,1,0:T(8,128)} async-done(((f32[4,128,128]{2,1,0:T(8,128)}), f32[4,128,128]{2,1,0:T(8,128)}) %all-reduce.2.cloned.1.call-update) | async-done | bytes 262160 | tf_op jit(solution)/shard_map/while/body/eval_jaxpr/psum | solution.py:12
  1538.4 37.2 %all-reduce.2.cloned.1.call-done = f32[4,128,128]{2,1,0:T(8,128)} async-done(((f32[4,128,128]{2,1,0:T(8,128)}), f32[4,128,128]{2,1,0:T(8,128)}) %all-reduce.2.cloned.1.call-update) | async-done | bytes 262160 | tf_op jit(solution)/shard_map/while/body/eval_jaxpr/psum | solution.py:12
  1636.0 37.5 %all-reduce.2.cloned.1.call-done = f32[4,128,128]{2,1,0:T(8,128)} async-done(((f32[4,128,128]{2,1,0:T(8,128)}), f32[4,128,128]{2,1,0:T(8,128)}) %all-reduce.2.cloned.1.call-update) | async-done | bytes 262160 | tf_op jit(solution)/shard_map/while/body/eval_jaxpr/psum | solution.py:12
  1733.7 37.5 %all-reduce.2.cloned.1.call-done = f32[4,128,128]{2,1,0:T(8,128)} async-done(((f32[4,128,128]{2,1,0:T(8,128)}), f32[4,128,128]{2,1,0:T(8,128)}) %all-reduce.2.cloned.1.call-update) | async-done | bytes 262160 | tf_op jit(solution)/shard_map/while/body/eval_jaxpr/psum | solution.py:12
  1830.9 81.8 %all-gather.10.cloned.1.call-done = f32[4,128,16,128]{3,1,2,0:T(8,128)} async-done(((f32[4,128,4,128]{3,1,2,0:T(8,128)}), f32[4,128,16,128]{3,1,2,0:T(8,128)}) %all-gather.10.cloned.1.call-update) | async-done | bytes 4194320 | tf_op jit(solution)/shard_map/all_gather | solution.py:94
  1916.5 39.8 %psum.21 = f32[16,128]{1,0:T(8,128)S(1)} all-reduce(f32[16,128]{1,0:T(8,128)S(1)} %fusion.18), channel_id=1, replica_groups=mesh['gx'=4,'gy'=4,'gz'=2] {'gx','gy','gz'}, use_global_device_ids=true, to_apply=%region_7.8 | all-reduce | flops 2048 | bytes 16384 | tf_op jit(solution)/shard_map/psum | solution.py:38
  1959.2 111.7 %all-gather.8.cloned.1.call-done = f32[4,4,128,4,4,128]{5,2,4,3,1,0:T(8,128)} async-done(((f32[1,4,128,4,4,128]{5,2,4,3,1,0:T(8,128)}), f32[4,4,128,4,4,128]{5,2,4,3,1,0:T(8,128)}) %all-gather.8.cloned.1.call-update) | async-done | bytes 16777232 | tf_op jit(solution)/shard_map/all_gather | solution.py:95
  2124.2 47.6 %while.19 = (s32[]{:T(128)}, f32[2048,2048]{1,0:T(8,128)}, s32[16,2]{0,1:T(2,128)S(1)}, f32[16,128,128]{2,1,0:T(8,128)S(1)}, s32[]{:T(128)}) while((s32[]{:T(128)}, f32[2048,2048]{1,0:T(8,128)}, s32[16,2]{0,1:T(2,128)S(1)}, f32[16,128,128]{2,1,0:T(8,128)S(1)}, s32[]{:T(128)}) %tuple.184), condition=%wide.while_cond, body=%wide.while_body.sunk | while | flops 2 | bytes 131181 | solution.py:98
  2171.8 157.4 %custom-call.28 = f32[16,128,128]{1,2,0:T(8,128)S(1)} custom-call(f32[16,128,128]{2,1,0:T(8,128)S(1)} %get-tuple-element.183), custom_call_target="InvertDiagBlocksLowerTriangular" | custom-call | tf_op jit(solution)/shard_map/jit(_solve_triangular)/triangular_solve | solution.py:98
  (583 shorter events, 1172.5 us)
Async XLA Ops:
  7.2 65.2 %reduce-scatter.3.cloned.1.call-start = ((), (), s32[]{:S(2)}) async-start(), calls=%async_computation.2 | async-start | bytes 25165824 | tf_op jit(solution)/shard_map/reduce_scatter | solution.py:43
  44.5 211.7 %reduce-scatter.5.cloned.1.call-start = ((), (), s32[]{:S(2)}) async-start(), calls=%async_computation.3 | async-start | bytes 8912896 | tf_op jit(solution)/shard_map/reduce_scatter | solution.py:44
  72.4 194.0 %all-gather.6.cloned.1.call-start = ((), (), s32[]{:S(2)}) async-start(), calls=%async_computation.4 | async-start | bytes 1572864 | tf_op jit(solution)/shard_map/all_gather | solution.py:45
  266.6 40.2 %all-reduce.2.cloned.1.call-start = ((), (), s32[]{:S(2)}) async-start(), calls=%async_computation.7 | async-start | bytes 524288 | tf_op jit(solution)/shard_map/while/body/eval_jaxpr/psum | solution.py:12
  268.4 66.4 %all-gather.12.cloned.1.call-start = ((), (), s32[]{:S(2)}) async-start(), calls=%async_computation.8 | async-start | bytes 1310720 | tf_op jit(solution)/shard_map/while/body/eval_jaxpr/all_gather | solution.py:63
  366.9 65.5 %all-gather.12.cloned.1.call-start = ((), (), s32[]{:S(2)}) async-start(), calls=%async_computation.8 | async-start | bytes 1310720 | tf_op jit(solution)/shard_map/while/body/eval_jaxpr/all_gather | solution.py:63
  464.5 65.8 %all-gather.12.cloned.1.call-start = ((), (), s32[]{:S(2)}) async-start(), calls=%async_computation.8 | async-start | bytes 1310720 | tf_op jit(solution)/shard_map/while/body/eval_jaxpr/all_gather | solution.py:63
  562.4 65.5 %all-gather.12.cloned.1.call-start = ((), (), s32[]{:S(2)}) async-start(), calls=%async_computation.8 | async-start | bytes 1310720 | tf_op jit(solution)/shard_map/while/body/eval_jaxpr/all_gather | solution.py:63
  660.0 65.5 %all-gather.12.cloned.1.call-start = ((), (), s32[]{:S(2)}) async-start(), calls=%async_computation.8 | async-start | bytes 1310720 | tf_op jit(solution)/shard_map/while/body/eval_jaxpr/all_gather | solution.py:63
  757.6 65.3 %all-gather.12.cloned.1.call-start = ((), (), s32[]{:S(2)}) async-start(), calls=%async_computation.8 | async-start | bytes 1310720 | tf_op jit(solution)/shard_map/while/body/eval_jaxpr/all_gather | solution.py:63
  855.0 65.3 %all-gather.12.cloned.1.call-start = ((), (), s32[]{:S(2)}) async-start(), calls=%async_computation.8 | async-start | bytes 1310720 | tf_op jit(solution)/shard_map/while/body/eval_jaxpr/all_gather | solution.py:63
  952.4 65.5 %all-gather.12.cloned.1.call-start = ((), (), s32[]{:S(2)}) async-start(), calls=%async_computation.8 | async-start | bytes 1310720 | tf_op jit(solution)/shard_map/while/body/eval_jaxpr/all_gather | solution.py:63
  1050.0 65.5 %all-gather.12.cloned.1.call-start = ((), (), s32[]{:S(2)}) async-start(), calls=%async_computation.8 | async-start | bytes 1310720 | tf_op jit(solution)/shard_map/while/body/eval_jaxpr/all_gather | solution.py:63
  1147.6 65.8 %all-gather.12.cloned.1.call-start = ((), (), s32[]{:S(2)}) async-start(), calls=%async_computation.8 | async-start | bytes 1310720 | tf_op jit(solution)/shard_map/while/body/eval_jaxpr/all_gather | solution.py:63
  1245.5 65.5 %all-gather.12.cloned.1.call-start = ((), (), s32[]{:S(2)}) async-start(), calls=%async_computation.8 | async-start | bytes 1310720 | tf_op jit(solution)/shard_map/while/body/eval_jaxpr/all_gather | solution.py:63
  1343.1 65.3 %all-gather.12.cloned.1.call-start = ((), (), s32[]{:S(2)}) async-start(), calls=%async_computation.8 | async-start | bytes 1310720 | tf_op jit(solution)/shard_map/while/body/eval_jaxpr/all_gather | solution.py:63
  1438.7 39.3 %all-reduce.2.cloned.1.call-start = ((), (), s32[]{:S(2)}) async-start(), calls=%async_computation.7 | async-start | bytes 524288 | tf_op jit(solution)/shard_map/while/body/eval_jaxpr/psum | solution.py:12
  1440.5 65.8 %all-gather.12.cloned.1.call-start = ((), (), s32[]{:S(2)}) async-start(), calls=%async_computation.8 | async-start | bytes 1310720 | tf_op jit(solution)/shard_map/while/body/eval_jaxpr/all_gather | solution.py:63
  1538.4 65.5 %all-gather.12.cloned.1.call-start = ((), (), s32[]{:S(2)}) async-start(), calls=%async_computation.8 | async-start | bytes 1310720 | tf_op jit(solution)/shard_map/while/body/eval_jaxpr/all_gather | solution.py:63
  1636.0 65.7 %all-gather.12.cloned.1.call-start = ((), (), s32[]{:S(2)}) async-start(), calls=%async_computation.8 | async-start | bytes 1310720 | tf_op jit(solution)/shard_map/while/body/eval_jaxpr/all_gather | solution.py:63
  1731.9 39.4 %all-reduce.2.cloned.1.call-start = ((), (), s32[]{:S(2)}) async-start(), calls=%async_computation.7 | async-start | bytes 524288 | tf_op jit(solution)/shard_map/while/body/eval_jaxpr/psum | solution.py:12
  1733.7 65.8 %all-gather.12.cloned.1.call-start = ((), (), s32[]{:S(2)}) async-start(), calls=%async_computation.8 | async-start | bytes 1310720 | tf_op jit(solution)/shard_map/while/body/eval_jaxpr/all_gather | solution.py:63
  1829.8 82.9 %all-gather.10.cloned.1.call-start = ((), (), s32[]{:S(2)}) async-start(), calls=%async_computation.6 | async-start | bytes 5242880 | tf_op jit(solution)/shard_map/all_gather | solution.py:94
  1830.8 240.1 %all-gather.8.cloned.1.call-start = ((), (), s32[]{:S(2)}) async-start(), calls=%async_computation.5 | async-start | bytes 20971520 | tf_op jit(solution)/shard_map/all_gather | solution.py:95
  (18 other events, 5451.5 us)
Sparse Core Ops, SparseCore 0:
  44.6 27.6 reduce-scatter.2
  74.6 181.5 reduce-scatter.4
  270.0 36.7 all-reduce.1
  368.6 35.5 all-reduce.1
  406.0 26.3 all-gather.11
  466.4 35.5 all-reduce.1
  503.9 26.3 all-gather.11
  564.0 35.5 all-reduce.1
  601.5 26.3 all-gather.11
  661.6 35.5 all-reduce.1
  699.1 26.3 all-gather.11
  759.2 35.5 all-reduce.1
  856.6 35.5 all-reduce.1
  954.0 35.5 all-reduce.1
  1051.6 35.5 all-reduce.1
  1149.5 35.5 all-reduce.1
  1247.1 35.5 all-reduce.1
  1344.7 35.5 all-reduce.1
  1442.4 35.5 all-reduce.1
  1540.0 35.5 all-reduce.1
  1637.9 35.5 all-reduce.1
  1735.6 35.5 all-reduce.1
  1831.9 80.7 all-gather.9
  1914.3 156.5 all-gather.7
  (13 shorter events, 324.2 us)
where the time goes:
time: 2400 us; the launch traced here: 2390 us
  waiting for transfers between devices  1460 us (61%)
  other arithmetic  584 us (24%)
  matrix products  154 us (6%)
  local copies, waits for them, and re-layouts  131 us (5%)
  blocking collectives  39.8 us (2%)
    psum x16, waiting for transfers between devices, from_root(): return lax.psum(block, axis)  598 us
    all_gather x16, waiting for transfers between devices, factor_step(): lax.all_gather(row_raw, 'gx', axis=0, tiled=True)  449 us
    another operation x48, other arithmetic, factor_step(): chol = jnp.linalg.cholesky(own_diag)  199 us
    reduce_scatter x1, waiting for transfers between devices, on_device(): lax.psum_scatter(halves, ('gx', 'gy'), scatter_dimension=0, tiled=True)  183 us
    another operation x3, other arithmetic, on_device(): jax.scipy.linalg.solve_triangular(lower, middle, lower=True, trans=1)  170 us
    another operation x32, other arithmetic, factor_step(): solved = jax.scipy.linalg.solve_triangular(chol, stacked, lower=True)  168 us
    all_gather x1, waiting for transfers between devices, on_device(): whole = lax.all_gather(across, 'gx', axis=0, tiled=True)  112 us
    all_gather x1, waiting for transfers between devices, on_device(): across = lax.all_gather(shaped, 'gy', axis=3, tiled=True)  81.8 us
  transfers between devices with their start and end apart: 37, of which 37 were waited for; matrix products, arithmetic and copies ran while one was open for 0% of the time, Pallas kernels for 0%

commit v1 on v0

--- a/solution.py
+++ b/solution.py
@@ -9,7 +9,7 @@
 
 def from_root(block, axis, source):
     block = jnp.where(lax.axis_index(axis) == source, block, jnp.zeros_like(block))
-    return lax.psum(block, axis)
+    return jax.lax.all_gather(block, axis).sum(axis=0)
 
 
 def on_device(blocks, coefficients, residuals):

time: 2400 us -> 2270 us (0.946)
  waiting for transfers between devices: 1460 us -> 1300 us
  other arithmetic: 584 us -> 614 us
    psum x16 -> x0, waiting for transfers between devices: 598 us -> none  [from_root(): return lax.psum(block, axis)]
    all_gather x0 -> x16, waiting for transfers between devices: none -> 464 us  [from_root(): return jax.lax.all_gather(block, axis).sum(axis=0)]
    reduce_sum x0 -> x16, other arithmetic: none -> 32.1 us  [from_root(): return jax.lax.all_gather(block, axis).sum(axis=0)]
    all_gather x16, waiting for transfers between devices: 449 us -> 419 us  [factor_step(): lax.all_gather(row_raw, 'gx', axis=0, tiled=True)]
where the time goes in v1:
time: 2270 us; the launch traced here: 2260 us
  waiting for transfers between devices  1300 us (57%)
  other arithmetic  614 us (27%)
  matrix products  154 us (7%)
  local copies, waits for them, and re-layouts  129 us (6%)
  blocking collectives  39.8 us (2%)
    all_gather x16, waiting for transfers between devices, from_root(): return jax.lax.all_gather(block, axis).sum(axis=0)  464 us
    all_gather x16, waiting for transfers between devices, factor_step(): lax.all_gather(row_raw, 'gx', axis=0, tiled=True)  419 us
    another operation x48, other arithmetic, factor_step(): chol = jnp.linalg.cholesky(own_diag)  198 us
    reduce_scatter x1, waiting for transfers between devices, on_device(): lax.psum_scatter(halves, ('gx', 'gy'), scatter_dimension=0, tiled=True)  183 us
    another operation x3, other arithmetic, on_device(): jax.scipy.linalg.solve_triangular(lower, middle, lower=True, trans=1)  170 us
    another operation x32, other arithmetic, factor_step(): solved = jax.scipy.linalg.solve_triangular(chol, stacked, lower=True)  167 us
    all_gather x1, waiting for transfers between devices, on_device(): whole = lax.all_gather(across, 'gx', axis=0, tiled=True)  112 us
    all_gather x1, waiting for transfers between devices, on_device(): across = lax.all_gather(shaped, 'gy', axis=3, tiled=True)  81.8 us
  transfers between devices with their start and end apart: 37, of which 37 were waited for; matrix products, arithmetic and copies ran while one was open for 0% of the time, Pallas kernels for 0%

profile of v1, /device:TPU:0, one launch (start us, length us, event | category | flops | bytes accessed | tf_op | source)
XLA Modules:
  0.0 2255.4 jit_solution(14142873615673086542)
XLA Ops:
  44.6 27.8 %reduce-scatter.3.cloned.1.call-done = f32[16,4,64,4,128]{4,2,3,1,0:T(8,128)} async-done(((f32[16,4,128,4,128]{4,2,3,1,0:T(8,128)}), f32[16,4,64,4,128]{4,2,3,1,0:T(8,128)}) %reduce-scatter.3.cloned.1.call-update) | async-done | bytes 8388624 | tf_op jit(solution)/shard_map/reduce_scatter | solution.py:43
  72.9 183.3 %reduce-scatter.5.cloned.1.call-done = f32[1,4,64,4,128]{4,2,3,1,0:T(8,128)} async-done(((f32[16,4,64,4,128]{4,2,3,1,0:T(8,128)}), f32[1,4,64,4,128]{4,2,3,1,0:T(8,128)}) %reduce-scatter.5.cloned.1.call-update) | async-done | bytes 524304 | tf_op jit(solution)/shard_map/reduce_scatter | solution.py:44
  266.6 1428.6 %while.20 = (s32[]{:T(128)}, f32[4,128,4,128]{3,1,2,0:T(8,128)}, f32[4,128,4,128]{3,1,2,0:T(8,128)S(1)}, s32[]{:T(128)}, s32[]{:T(128)}, /*index=5*/s32[]{:T(128...) while((s32[]{:T(128)}, f32[4,128,4,128]{3,1,2,0:T(8,128)}, ...), condition=%wide.region_6.7_spmd.clone, body=%wide.region_2.6_spmd.clone.sunk | while | flops 806437056 | bytes 16058448 | solution.py:92
  268.5 29.9 %all-gather.17.cloned.1.call-done = f32[16,128,1,128]{3,1,2,0:T(8,128)} async-done(((f32[4,128,1,128]{3,1,2,0:T(8,128)}), f32[16,128,1,128]{3,1,2,0:T(8,128)}) %all-gather.17.cloned.1.call-update) | async-done | bytes 1048592 | tf_op jit(solution)/shard_map/while/body/eval_jaxpr/all_gather | solution.py:12
  358.6 28.8 %all-gather.17.cloned.1.call-done = f32[16,128,1,128]{3,1,2,0:T(8,128)} async-done(((f32[4,128,1,128]{3,1,2,0:T(8,128)}), f32[16,128,1,128]{3,1,2,0:T(8,128)}) %all-gather.17.cloned.1.call-update) | async-done | bytes 1048592 | tf_op jit(solution)/shard_map/while/body/eval_jaxpr/all_gather | solution.py:12
  447.7 29.1 %all-gather.17.cloned.1.call-done = f32[16,128,1,128]{3,1,2,0:T(8,128)} async-done(((f32[4,128,1,128]{3,1,2,0:T(8,128)}), f32[16,128,1,128]{3,1,2,0:T(8,128)}) %all-gather.17.cloned.1.call-update) | async-done | bytes 1048592 | tf_op jit(solution)/shard_map/while/body/eval_jaxpr/all_gather | solution.py:12
  537.2 28.8 %all-gather.17.cloned.1.call-done = f32[16,128,1,128]{3,1,2,0:T(8,128)} async-done(((f32[4,128,1,128]{3,1,2,0:T(8,128)}), f32[16,128,1,128]{3,1,2,0:T(8,128)}) %all-gather.17.cloned.1.call-update) | async-done | bytes 1048592 | tf_op jit(solution)/shard_map/while/body/eval_jaxpr/all_gather | solution.py:12
  626.4 28.8 %all-gather.17.cloned.1.call-done = f32[16,128,1,128]{3,1,2,0:T(8,128)} async-done(((f32[4,128,1,128]{3,1,2,0:T(8,128)}), f32[16,128,1,128]{3,1,2,0:T(8,128)}) %all-gather.17.cloned.1.call-update) | async-done | bytes 1048592 | tf_op jit(solution)/shard_map/while/body/eval_jaxpr/all_gather | solution.py:12
  715.6 28.8 %all-gather.17.cloned.1.call-done = f32[16,128,1,128]{3,1,2,0:T(8,128)} async-done(((f32[4,128,1,128]{3,1,2,0:T(8,128)}), f32[16,128,1,128]{3,1,2,0:T(8,128)}) %all-gather.17.cloned.1.call-update) | async-done | bytes 1048592 | tf_op jit(solution)/shard_map/while/body/eval_jaxpr/all_gather | solution.py:12
  804.6 28.8 %all-gather.17.cloned.1.call-done = f32[16,128,1,128]{3,1,2,0:T(8,128)} async-done(((f32[4,128,1,128]{3,1,2,0:T(8,128)}), f32[16,128,1,128]{3,1,2,0:T(8,128)}) %all-gather.17.cloned.1.call-update) | async-done | bytes 1048592 | tf_op jit(solution)/shard_map/while/body/eval_jaxpr/all_gather | solution.py:12
  893.6 28.8 %all-gather.17.cloned.1.call-done = f32[16,128,1,128]{3,1,2,0:T(8,128)} async-done(((f32[4,128,1,128]{3,1,2,0:T(8,128)}), f32[16,128,1,128]{3,1,2,0:T(8,128)}) %all-gather.17.cloned.1.call-update) | async-done | bytes 1048592 | tf_op jit(solution)/shard_map/while/body/eval_jaxpr/all_gather | solution.py:12
  982.7 28.8 %all-gather.17.cloned.1.call-done = f32[16,128,1,128]{3,1,2,0:T(8,128)} async-done(((f32[4,128,1,128]{3,1,2,0:T(8,128)}), f32[16,128,1,128]{3,1,2,0:T(8,128)}) %all-gather.17.cloned.1.call-update) | async-done | bytes 1048592 | tf_op jit(solution)/shard_map/while/body/eval_jaxpr/all_gather | solution.py:12
  1071.9 29.1 %all-gather.17.cloned.1.call-done = f32[16,128,1,128]{3,1,2,0:T(8,128)} async-done(((f32[4,128,1,128]{3,1,2,0:T(8,128)}), f32[16,128,1,128]{3,1,2,0:T(8,128)}) %all-gather.17.cloned.1.call-update) | async-done | bytes 1048592 | tf_op jit(solution)/shard_map/while/body/eval_jaxpr/all_gather | solution.py:12
  1161.4 28.8 %all-gather.17.cloned.1.call-done = f32[16,128,1,128]{3,1,2,0:T(8,128)} async-done(((f32[4,128,1,128]{3,1,2,0:T(8,128)}), f32[16,128,1,128]{3,1,2,0:T(8,128)}) %all-gather.17.cloned.1.call-update) | async-done | bytes 1048592 | tf_op jit(solution)/shard_map/while/body/eval_jaxpr/all_gather | solution.py:12
  1250.6 28.8 %all-gather.17.cloned.1.call-done = f32[16,128,1,128]{3,1,2,0:T(8,128)} async-done(((f32[4,128,1,128]{3,1,2,0:T(8,128)}), f32[16,128,1,128]{3,1,2,0:T(8,128)}) %all-gather.17.cloned.1.call-update) | async-done | bytes 1048592 | tf_op jit(solution)/shard_map/while/body/eval_jaxpr/all_gather | solution.py:12
  1339.6 29.2 %all-gather.17.cloned.1.call-done = f32[16,128,1,128]{3,1,2,0:T(8,128)} async-done(((f32[4,128,1,128]{3,1,2,0:T(8,128)}), f32[16,128,1,128]{3,1,2,0:T(8,128)}) %all-gather.17.cloned.1.call-update) | async-done | bytes 1048592 | tf_op jit(solution)/shard_map/while/body/eval_jaxpr/all_gather | solution.py:12
  1429.1 28.8 %all-gather.17.cloned.1.call-done = f32[16,128,1,128]{3,1,2,0:T(8,128)} async-done(((f32[4,128,1,128]{3,1,2,0:T(8,128)}), f32[16,128,1,128]{3,1,2,0:T(8,128)}) %all-gather.17.cloned.1.call-update) | async-done | bytes 1048592 | tf_op jit(solution)/shard_map/while/body/eval_jaxpr/all_gather | solution.py:12
  1518.2 29.1 %all-gather.17.cloned.1.call-done = f32[16,128,1,128]{3,1,2,0:T(8,128)} async-done(((f32[4,128,1,128]{3,1,2,0:T(8,128)}), f32[16,128,1,128]{3,1,2,0:T(8,128)}) %all-gather.17.cloned.1.call-update) | async-done | bytes 1048592 | tf_op jit(solution)/shard_map/while/body/eval_jaxpr/all_gather | solution.py:12
  1607.6 29.1 %all-gather.17.cloned.1.call-done = f32[16,128,1,128]{3,1,2,0:T(8,128)} async-done(((f32[4,128,1,128]{3,1,2,0:T(8,128)}), f32[16,128,1,128]{3,1,2,0:T(8,128)}) %all-gather.17.cloned.1.call-update) | async-done | bytes 1048592 | tf_op jit(solution)/shard_map/while/body/eval_jaxpr/all_gather | solution.py:12
  1696.3 81.8 %all-gather.15.cloned.1.call-done = f32[4,128,16,128]{3,1,2,0:T(8,128)} async-done(((f32[4,128,4,128]{3,1,2,0:T(8,128)}), f32[4,128,16,128]{3,1,2,0:T(8,128)}) %all-gather.15.cloned.1.call-update) | async-done | bytes 4194320 | tf_op jit(solution)/shard_map/all_gather | solution.py:94
  1781.9 39.8 %psum.7 = f32[16,128]{1,0:T(8,128)S(1)} all-reduce(f32[16,128]{1,0:T(8,128)S(1)} %fusion.19), channel_id=1, replica_groups=mesh['gx'=4,'gy'=4,'gz'=2] {'gx','gy','gz'}, use_global_device_ids=true, to_apply=%region_7.8 | all-reduce | flops 2048 | bytes 16384 | tf_op jit(solution)/shard_map/psum | solution.py:38
  1824.6 111.7 %all-gather.13.cloned.1.call-done = f32[4,4,128,4,4,128]{5,2,4,3,1,0:T(8,128)} async-done(((f32[1,4,128,4,4,128]{5,2,4,3,1,0:T(8,128)}), f32[4,4,128,4,4,128]{5,2,4,3,1,0:T(8,128)}) %all-gather.13.cloned.1.call-update) | async-done | bytes 16777232 | tf_op jit(solution)/shard_map/all_gather | solution.py:95
  1989.6 47.6 %while.19 = (s32[]{:T(128)}, f32[2048,2048]{1,0:T(8,128)}, s32[16,2]{0,1:T(2,128)S(1)}, f32[16,128,128]{2,1,0:T(8,128)S(1)}, s32[]{:T(128)}) while((s32[]{:T(128)}, f32[2048,2048]{1,0:T(8,128)}, s32[16,2]{0,1:T(2,128)S(1)}, f32[16,128,128]{2,1,0:T(8,128)S(1)}, s32[]{:T(128)}) %tuple.184), condition=%wide.while_cond, body=%wide.while_body.sunk | while | flops 2 | bytes 131181 | solution.py:98
  2037.2 157.4 %custom-call.28 = f32[16,128,128]{1,2,0:T(8,128)S(1)} custom-call(f32[16,128,128]{2,1,0:T(8,128)S(1)} %get-tuple-element.183), custom_call_target="InvertDiagBlocksLowerTriangular" | custom-call | tf_op jit(solution)/shard_map/jit(_solve_triangular)/triangular_solve | solution.py:98
  (583 shorter events, 1172.2 us)
Async XLA Ops:
  7.2 65.2 %reduce-scatter.3.cloned.1.call-start = ((), (), s32[]{:S(2)}) async-start(), calls=%async_computation.2 | async-start | bytes 25165824 | tf_op jit(solution)/shard_map/reduce_scatter | solution.py:43
  44.5 211.7 %reduce-scatter.5.cloned.1.call-start = ((), (), s32[]{:S(2)}) async-start(), calls=%async_computation.3 | async-start | bytes 8912896 | tf_op jit(solution)/shard_map/reduce_scatter | solution.py:44
  72.4 194.0 %all-gather.11.cloned.1.call-start = ((), (), s32[]{:S(2)}) async-start(), calls=%async_computation.4 | async-start | bytes 1572864 | tf_op jit(solution)/shard_map/all_gather | solution.py:45
  266.6 31.8 %all-gather.17.cloned.1.call-start = ((), (), s32[]{:S(2)}) async-start(), calls=%async_computation.7 | async-start | bytes 1310720 | tf_op jit(solution)/shard_map/while/body/eval_jaxpr/all_gather | solution.py:12
  268.4 58.2 %all-gather.19.cloned.1.call-start = ((), (), s32[]{:S(2)}) async-start(), calls=%async_computation.8 | async-start | bytes 1310720 | tf_op jit(solution)/shard_map/while/body/eval_jaxpr/all_gather | solution.py:63
  358.5 57.2 %all-gather.19.cloned.1.call-start = ((), (), s32[]{:S(2)}) async-start(), calls=%async_computation.8 | async-start | bytes 1310720 | tf_op jit(solution)/shard_map/while/body/eval_jaxpr/all_gather | solution.py:63
  447.7 57.5 %all-gather.19.cloned.1.call-start = ((), (), s32[]{:S(2)}) async-start(), calls=%async_computation.8 | async-start | bytes 1310720 | tf_op jit(solution)/shard_map/while/body/eval_jaxpr/all_gather | solution.py:63
  537.2 57.2 %all-gather.19.cloned.1.call-start = ((), (), s32[]{:S(2)}) async-start(), calls=%async_computation.8 | async-start | bytes 1310720 | tf_op jit(solution)/shard_map/while/body/eval_jaxpr/all_gather | solution.py:63
  626.3 57.2 %all-gather.19.cloned.1.call-start = ((), (), s32[]{:S(2)}) async-start(), calls=%async_computation.8 | async-start | bytes 1310720 | tf_op jit(solution)/shard_map/while/body/eval_jaxpr/all_gather | solution.py:63
  715.5 57.0 %all-gather.19.cloned.1.call-start = ((), (), s32[]{:S(2)}) async-start(), calls=%async_computation.8 | async-start | bytes 1310720 | tf_op jit(solution)/shard_map/while/body/eval_jaxpr/all_gather | solution.py:63
  804.5 57.0 %all-gather.19.cloned.1.call-start = ((), (), s32[]{:S(2)}) async-start(), calls=%async_computation.8 | async-start | bytes 1310720 | tf_op jit(solution)/shard_map/while/body/eval_jaxpr/all_gather | solution.py:63
  893.5 57.2 %all-gather.19.cloned.1.call-start = ((), (), s32[]{:S(2)}) async-start(), calls=%async_computation.8 | async-start | bytes 1310720 | tf_op jit(solution)/shard_map/while/body/eval_jaxpr/all_gather | solution.py:63
  982.7 57.2 %all-gather.19.cloned.1.call-start = ((), (), s32[]{:S(2)}) async-start(), calls=%async_computation.8 | async-start | bytes 1310720 | tf_op jit(solution)/shard_map/while/body/eval_jaxpr/all_gather | solution.py:63
  1070.1 31.0 %all-gather.17.cloned.1.call-start = ((), (), s32[]{:S(2)}) async-start(), calls=%async_computation.7 | async-start | bytes 1310720 | tf_op jit(solution)/shard_map/while/body/eval_jaxpr/all_gather | solution.py:12
  1071.9 57.5 %all-gather.19.cloned.1.call-start = ((), (), s32[]{:S(2)}) async-start(), calls=%async_computation.8 | async-start | bytes 1310720 | tf_op jit(solution)/shard_map/while/body/eval_jaxpr/all_gather | solution.py:63
  1161.4 57.2 %all-gather.19.cloned.1.call-start = ((), (), s32[]{:S(2)}) async-start(), calls=%async_computation.8 | async-start | bytes 1310720 | tf_op jit(solution)/shard_map/while/body/eval_jaxpr/all_gather | solution.py:63
  1250.5 57.0 %all-gather.19.cloned.1.call-start = ((), (), s32[]{:S(2)}) async-start(), calls=%async_computation.8 | async-start | bytes 1310720 | tf_op jit(solution)/shard_map/while/body/eval_jaxpr/all_gather | solution.py:63
  1337.7 31.0 %all-gather.17.cloned.1.call-start = ((), (), s32[]{:S(2)}) async-start(), calls=%async_computation.7 | async-start | bytes 1310720 | tf_op jit(solution)/shard_map/while/body/eval_jaxpr/all_gather | solution.py:12
  1339.5 57.5 %all-gather.19.cloned.1.call-start = ((), (), s32[]{:S(2)}) async-start(), calls=%async_computation.8 | async-start | bytes 1310720 | tf_op jit(solution)/shard_map/while/body/eval_jaxpr/all_gather | solution.py:63
  1429.0 57.2 %all-gather.19.cloned.1.call-start = ((), (), s32[]{:S(2)}) async-start(), calls=%async_computation.8 | async-start | bytes 1310720 | tf_op jit(solution)/shard_map/while/body/eval_jaxpr/all_gather | solution.py:63
  1518.2 57.4 %all-gather.19.cloned.1.call-start = ((), (), s32[]{:S(2)}) async-start(), calls=%async_computation.8 | async-start | bytes 1310720 | tf_op jit(solution)/shard_map/while/body/eval_jaxpr/all_gather | solution.py:63
  1607.5 57.5 %all-gather.19.cloned.1.call-start = ((), (), s32[]{:S(2)}) async-start(), calls=%async_computation.8 | async-start | bytes 1310720 | tf_op jit(solution)/shard_map/while/body/eval_jaxpr/all_gather | solution.py:63
  1695.2 82.8 %all-gather.15.cloned.1.call-start = ((), (), s32[]{:S(2)}) async-start(), calls=%async_computation.6 | async-start | bytes 5242880 | tf_op jit(solution)/shard_map/all_gather | solution.py:94
  1696.2 240.1 %all-gather.13.cloned.1.call-start = ((), (), s32[]{:S(2)}) async-start(), calls=%async_computation.5 | async-start | bytes 20971520 | tf_op jit(solution)/shard_map/all_gather | solution.py:95
  (18 other events, 4938.8 us)
Sparse Core Ops, SparseCore 0:
  44.6 27.6 reduce-scatter.2
  74.6 181.5 reduce-scatter.4
  269.2 29.1 all-gather.16
  300.7 25.8 all-gather.18
  359.4 27.9 all-gather.16
  448.9 27.9 all-gather.16
  479.3 25.8 all-gather.18
  538.0 27.9 all-gather.16
  627.2 27.9 all-gather.16
  716.4 27.9 all-gather.16
  746.6 25.8 all-gather.18
  805.4 27.9 all-gather.16
  835.7 25.8 all-gather.18
  894.4 27.9 all-gather.16
  983.6 27.9 all-gather.16
  1073.0 27.9 all-gather.16
  1162.2 27.9 all-gather.16
  1251.4 27.9 all-gather.16
  1340.7 27.9 all-gather.16
  1429.9 27.9 all-gather.16
  1519.4 27.9 all-gather.16
  1608.7 27.9 all-gather.16
  1697.3 80.7 all-gather.14
  1779.7 156.5 all-gather.12
  (13 shorter events, 318.3 us)
